TPU v7x, 256 devices: a whole 4x4x8 slice. The times are simulated.
256 devices in a mesh: gx: 32 (over x_hi, z, core), gy: 8 (over y, x_lo).
Axes of the slice: x: 4 (x_hi: 2, x_lo: 2; x = x_hi * 2 + x_lo), y: 4, z: 8, core: 2. Of those that a mesh axis runs over, the one named last changes fastest.
Arguments:
- density: float32 [64, 24, 27648], P('gx', None, 'gy'), may hold values from 0.05 to 1
- gains_a: float32 [8, 24, 24, 24], replicated, may hold values from -6 to 6
- gains_b: float32 [8, 24, 24, 24], replicated, may hold values from -6 to 6
- loss_rates: float32 [24, 24, 24], replicated, may hold values from 0.1 to 1
Outputs:
- evolved: float32 [64, 24, 27648], P('gx', None, 'gy')
All inputs are finite; a program needn't handle non-finite values.
Results may differ from a plain program's by a relative error of at most 0.0001.
Values sent between devices are 32-bit elements; how exact they have to be, the bound alone decides.
A program may use at most 128 MiB of HBM per device.

v0:
```python
import functools

import jax
import jax.numpy as jnp
import numpy as np
from jax import lax
from jax.experimental import pallas as pl
from jax.experimental.pallas import tpu as pltpu
from jax.sharding import PartitionSpec as P

COUNT = 24
HALF = COUNT // 2
PLACES = HALF * HALF
LANES = 128
CELLS = 4
CHUNK = 16
collide_step = 0.2
courant_max = 1.6
f32 = jnp.float32


def cosine_table():
    freq = np.arange(COUNT)[:, None]
    points = np.arange(COUNT)[None, :]
    scale = np.where(freq == 0, np.sqrt(1.0 / COUNT), np.sqrt(2.0 / COUNT))
    return scale * np.cos(np.pi * (2 * points + 1) * freq / (2 * COUNT))


def two_parts(table):
    high = table.astype(jnp.bfloat16)
    return high, (table - high.astype(np.float64)).astype(jnp.bfloat16)


def transform_tables():
    cosine = cosine_table()
    plane = []
    for parity_x in range(2):
        for parity_y in range(2):
            along_x, along_y = cosine[parity_x::2, :HALF], cosine[parity_y::2, :HALF]
            plane.append(np.einsum("jn,lm->mnjl", along_x, along_y).reshape(PLACES, PLACES))
    plane = np.stack(plane)

    def stacked(table):
        return np.concatenate(two_parts(table), 1)

    def line(table):
        used = CELLS * COUNT
        wide = np.zeros((LANES, LANES))
        wide[:used, :used] = np.kron(np.eye(CELLS), table)
        high, low = two_parts(wide)
        return np.block([[high, low], [high, np.zeros_like(high)]])

    return stacked(plane.transpose(0, 2, 1)), line(cosine.T), stacked(plane), line(cosine)


def weights():
    speeds = np.arange(COUNT) - (COUNT - 1) / 2
    numbers = courant_max * np.abs(speeds) / ((COUNT - 1) / 2)
    return np.stack([1 - 1.5 * numbers + 0.5 * numbers**2, 2 * numbers - numbers**2, 0.5 * (numbers**2 - numbers)])


def x_weights():
    return np.broadcast_to(weights().reshape(3, 2, HALF, 1), (3, 2, HALF, LANES)).astype(np.float32)


def y_weights():
    both = weights().reshape(3, 2, HALF)
    both = np.stack([both[:, 0], both[:, 1, ::-1]], 1)
    both = np.repeat(both, HALF, 2)[..., None]
    return np.broadcast_to(both, (3, 2, PLACES, LANES)).astype(np.float32)


def split(value):
    high = value.astype(jnp.bfloat16)
    return high, (value - high.astype(f32)).astype(jnp.bfloat16)


def line_transform(value, table):
    both = jnp.dot(jnp.concatenate(split(value), 1), table, preferred_element_type=f32)
    return both[:, :LANES] + both[:, LANES:]


def plane_transform(value, table):
    high, low = split(value)
    first = jnp.dot(table, high, preferred_element_type=f32)
    second = jnp.dot(table[:PLACES], low, preferred_element_type=f32)
    return first[:PLACES] + first[PLACES:] + second


def butterfly(parts):
    sum_0, diff_0 = parts[0] + parts[1], parts[0] - parts[1]
    sum_1, diff_1 = parts[2] + parts[3], parts[2] - parts[3]
    return sum_0 + sum_1, diff_0 + diff_1, sum_0 - sum_1, diff_0 - diff_1


def block(index):
    return slice(index * LANES, (index + 1) * LANES)


def side_by_side(value, parts):
    return jnp.concatenate([value[i * PLACES : (i + 1) * PLACES] for i in range(parts)], 1)


def backward(groups, factors, modes, mixed, plane, line):
    for q in range(4):
        scaled = [modes[q, :, block(g)] * factor(q) for factor in factors for g in range(groups)]
        moved = line_transform(jnp.concatenate(scaled, 0), line[...])
        mixed[q, :, : len(scaled) * LANES] = plane_transform(side_by_side(moved, len(scaled)), plane[q])


def forward(groups, field, modes, mixed, plane, line):
    wide = groups * LANES
    for start in range(0, PLACES, CHUNK):
        rows = slice(start, start + CHUNK)
        parts = butterfly([field[q, rows, :] for q in range(4)])
        for q in range(4):
            mixed[q, rows, :wide] = parts[q]
    for q in range(4):
        moved = plane_transform(mixed[q, :, :wide], plane[q])
        stacked = jnp.concatenate([moved[:, block(g)] for g in range(groups)], 0)
        modes[q] = side_by_side(line_transform(stacked, line[...]), groups)


def collide_term(groups, field, total, modes, mixed, gain_a, gain_b, loss, tables):
    plane_fwd, line_fwd, plane_back, line_back = tables
    wide = groups * LANES

    @pl.when(pl.program_id(0) == 0)
    def _():
        forward(groups, field, modes, mixed, plane_fwd, line_fwd)
        backward(groups, [lambda q: loss[q]], modes, mixed, plane_back, line_back)
        for start in range(0, PLACES, CHUNK):
            rows = slice(start, start + CHUNK)
            parts = butterfly([mixed[q, rows, :wide] for q in range(4)])
            for q in range(4):
                total[q, rows, :] = -field[q, rows, :] * parts[q]

    backward(groups, [lambda q: gain_a[0, q], lambda q: gain_b[0, q]], modes, mixed, plane_back, line_back)
    for start in range(0, PLACES, CHUNK):
        rows = slice(start, start + CHUNK)
        first = butterfly([mixed[q, rows, :wide] for q in range(4)])
        second = butterfly([mixed[q, rows, wide : 2 * wide] for q in range(4)])
        for q in range(4):
            total[q, rows, :] += first[q] * second[q]


def piece(y, cell_x, cell_y):
    return cell_y * COUNT * COUNT + y * COUNT


def x_kernel(groups, density, below, above, weight, gain_a, gain_b, loss, *refs):
    tables, (out, lower, upper, swept, field, total, modes, mixed) = refs[:4], refs[4:]

    @pl.when(pl.program_id(0) == 0)
    def _():
        neg = [density[c, :HALF, :] for c in range(2)] + [above[:HALF, :], above[HALF:, :]]
        nw = [weight[k, 0, :, :1] for k in range(3)]
        for c in range(2):
            swept[c, 0, :HALF, :] = nw[0] * neg[c] + nw[1] * neg[c + 1] + nw[2] * neg[c + 2]
        pos = [below[:HALF, :], below[HALF:, :]] + [density[c, HALF:, :] for c in range(2)]
        pw = [weight[k, 1, :, :1] for k in range(3)]
        for c in range(2):
            new = pw[0] * pos[c + 2] + pw[1] * pos[c + 1] + pw[2] * pos[c]
            for row in range(HALF):
                swept[c, 1, HALF - 1 - row : HALF - row, :] = new[row : row + 1]
        for half_y in range(2):
            for place in range(HALF):
                y = COUNT - 1 - place if half_y else place
                for half_x in range(2):
                    for g in range(groups):
                        parts = []
                        for s in range(CELLS):
                            at = piece(y, s // 2, 2 * g + s % 2)
                            parts.append(swept[s // 2, half_x, :HALF, at : at + COUNT])
                        parts.append(jnp.zeros((HALF, LANES - CELLS * COUNT), f32))
                        field[2 * half_x + half_y, place * HALF : (place + 1) * HALF, block(g)] = jnp.concatenate(parts, 1)

    collide_term(groups, field, total, modes, mixed, gain_a, gain_b, loss, tables)

    @pl.when(pl.program_id(0) == pl.num_programs(0) - 1)
    def _():
        for q in range(4):
            out[q] = field[q] + collide_step * total[q]
        for half_x in range(2):
            lower[half_x] = out[2 * half_x, :, block(0)]
            upper[half_x] = out[2 * half_x + 1, :, block(groups - 1)]


def y_kernel(groups, before, below, above, weight, gain_a, gain_b, loss, *refs):
    tables, (out, swept, field, total, modes, mixed) = refs[:4], refs[4:]

    @pl.when(pl.program_id(0) == 0)
    def _():
        place = lax.broadcasted_iota(jnp.int32, (PLACES, LANES), 1) // COUNT
        odd = place % 2 == 1
        for half_x in range(2):
            for half_y in range(2):
                q = 2 * half_x + half_y
                w0, w1, w2 = [weight[k, half_y] for k in range(3)]
                blocks = [before[q, :, block(g)] for g in range(groups)]
                blocks = [below[half_x]] + blocks if half_y else blocks + [above[half_x]]
                right = [pltpu.roll(b, COUNT, 1) for b in blocks]
                left = [pltpu.roll(b, LANES - COUNT, 1) for b in blocks]
                for g in range(groups):
                    if half_y:
                        near = jnp.where(odd, right[g + 1], left[g])
                        new = w0 * blocks[g + 1] + w1 * near + w2 * blocks[g]
                    else:
                        near = jnp.where(odd, right[g + 1], left[g])
                        new = w0 * blocks[g] + w1 * near + w2 * blocks[g + 1]
                    field[q, :, block(g)] = new

    collide_term(groups, field, total, modes, mixed, gain_a, gain_b, loss, tables)

    @pl.when(pl.program_id(0) == pl.num_programs(0) - 1)
    def _():
        for q in range(4):
            field[q] = field[q] + collide_step * total[q]
        for half_x in range(2):
            for c in range(2):
                for g in range(groups):
                    parts = []
                    for cell_y in range(2):
                        for y in range(COUNT):
                            half_y, place = (0, y) if y < HALF else (1, COUNT - 1 - y)
                            at = g * LANES + (2 * c + cell_y) * COUNT
                            parts.append(field[2 * half_x + half_y, place * HALF : (place + 1) * HALF, at : at + COUNT])
                    wide = 2 * COUNT * COUNT
                    swept[c, half_x, :HALF, g * wide : (g + 1) * wide] = jnp.concatenate(parts, 1)
        for c in range(2):
            out[c, :HALF, :] = swept[c, 0, :HALF, :]
            for row in range(HALF):
                out[c, HALF + row : HALF + row + 1, :] = swept[c, 1, HALF - 1 - row : HALF - row, :]


def whole(array):
    return pl.BlockSpec(array.shape, lambda p: (0,) * array.ndim)


def call(kernel, groups, terms, field_args, gains, tables, out_shapes, scratch):
    gain = pl.BlockSpec((1, 4, PLACES, LANES), lambda p: (p, 0, 0, 0))
    wide = groups * LANES
    return pl.pallas_call(
        functools.partial(kernel, groups),
        grid=(terms,),
        out_shape=out_shapes,
        in_specs=[whole(a) for a in field_args] + [gain, gain, whole(gains[2])] + [whole(t) for t in tables],
        out_specs=jax.tree.map(whole, out_shapes),
        scratch_shapes=scratch
        + [pltpu.VMEM((4, PLACES, n * wide), f32) for n in (1, 1, 1, 2)],
    )(*field_args, *gains, *tables)


def by_parity(factor):
    terms = factor.shape[0]
    factor = factor.reshape(terms, HALF, 2, HALF, 2, COUNT).transpose(0, 2, 4, 1, 3, 5).reshape(terms, 4, PLACES, COUNT)
    return jnp.pad(jnp.concatenate([factor] * CELLS, -1), ((0, 0),) * 3 + ((0, LANES - CELLS * COUNT),))


def passed_along(value, axis, steps):
    count = lax.axis_size(axis)
    pairs = [(source, (source + steps) % count) for source in range(count)]
    return lax.ppermute(value, axis, pairs)


def body(density, gains_a, gains_b, loss_rates):
    cells_x, count, merged = density.shape
    terms = gains_a.shape[0]
    groups = merged // (2 * count * count)
    below = passed_along(density[:, HALF:].reshape(count, merged), "gx", 1)
    above = passed_along(density[:, :HALF].reshape(count, merged), "gx", -1)
    gains = (by_parity(gains_a), by_parity(gains_b), by_parity(loss_rates[None])[0])
    tables = tuple(jnp.asarray(t) for t in transform_tables())
    inner = jax.ShapeDtypeStruct((4, PLACES, groups * LANES), f32)
    rim = jax.ShapeDtypeStruct((2, PLACES, LANES), f32)
    swept = pltpu.VMEM((2, 2, 16, merged), f32)
    field, lower, upper = call(
        x_kernel, groups, terms, (density, below, above, jnp.asarray(x_weights())), gains, tables, (inner, rim, rim), [swept]
    )
    below = passed_along(upper, "gy", 1)
    above = passed_along(lower, "gy", -1)
    out = jax.ShapeDtypeStruct(density.shape, f32)
    return call(y_kernel, groups, terms, (field, below, above, jnp.asarray(y_weights())), gains, tables, out, [swept])


def solution(mesh):
    in_specs = (P("gx", None, "gy"), P(), P(), P())
    out_specs = P("gx", None, "gy")
    return jax.shard_map(body, mesh=mesh, in_specs=in_specs, out_specs=out_specs, check_vma=False)
```

profile of v0, /device:TPU:26, one launch (start us, length us, event | category | flops | bytes accessed | tf_op | source)
XLA Modules:
  0.0 73.6 jit_solution(2787334072333618377)
XLA Ops:
  0.0 0.0 copy-start
  0.0 1.4 %fusion.1 = (f32[2,12,3456]{2,1,0:T(8,128)S(1)}, f32[2,12,3456]{2,1,0:T(8,128)S(1)}) fusion(f32[2,24,3456]{2,1,0:T(8,128)} %density.1), kind=kLoop, calls=%fused_computation.12 | loop fusion | bytes 1327104 | tf_op jit(solution)/shard_map/slice | solution.py:271
  1.4 0.8 %reshape.21 = f32[24,3456]{1,0:T(8,128)} reshape(f32[2,12,3456]{2,1,0:T(8,128)S(1)} %get-tuple-element.12) | data formatting | bytes 663552 | tf_op jit(solution)/shard_map/reshape | solution.py:270
  2.1 0.0 collective-permute-start
  2.2 6.9 %collective-permute-start.1 = (f32[24,3456]{1,0:T(8,128)S(1)}, f32[24,3456]{1,0:T(8,128)S(1)}, u32[]{:S(2)}, u32[]{:S(2)}) collective-permute-start(f32[24,3456]{1,0:T(8,128)S(1)} %reshape.22), channel_id=1, source_target_pairs={{0,248},{8,0},{16,8},{24,16},{32,24},{40,32},{48,40},{56,48},{64,5... | collective-permute-start | bytes 995336 | tf_op jit(solution)/shard_map/ppermute | solution.py:263
  9.1 0.0 copy-done
  9.1 1.4 %copy.14 = f32[8,12,2,12,2,24]{5,0,3,1,4,2:T(8,128)S(1)} copy(f32[8,12,2,12,2,24]{5,4,3,2,1,0:T(2,128)S(1)} %bitcast.16) | data formatting | bytes 884736 | tf_op jit(solution)/shard_map/reshape | solution.py:256
  10.5 0.0 copy-start.1
  10.5 0.5 copy.15
  11.0 1.2 %copy-done.1 = f32[8,24,24,24]{3,2,1,0:T(8,128)S(1)} copy-done((f32[8,24,24,24]{3,2,1,0:T(8,128)S(1)}, f32[8,24,24,24]{3,2,1,0:T(8,128)}, u32[]{:S(2)}) %copy-start.1) | copy-done | bytes 442392
  12.1 1.4 %copy.19 = f32[8,12,2,12,2,24]{5,0,3,1,4,2:T(8,128)S(1)} copy(f32[8,12,2,12,2,24]{5,4,3,2,1,0:T(2,128)S(1)} %bitcast.17) | data formatting | bytes 884736 | tf_op jit(solution)/shard_map/reshape | solution.py:256
  13.5 0.0 copy-start.4
  13.5 0.5 copy.20
  14.0 0.5 copy-done.4
  14.5 0.1 copy.24
  14.6 1.0 %fusion.loss = f32[4,144,128]{2,1,0:T(8,128)} fusion(f32[1,4,144,24]{3,2,1,0:T(8,128)S(1)} %copy.25), kind=kLoop, calls=%fused_computation.8 | loop fusion | flops 589824 | bytes 350208 | tf_op jit(solution)/shard_map/squeeze | solution.py:272
  15.6 5.2 %select_maximum_fusion = (f32[8,4,144,128]{3,2,1,0:T(8,128)}, f32[8,4,144,128]{3,2,1,0:T(8,128)}) fusion(f32[8,4,144,24]{3,2,1,0:T(8,128)S(1)} %copy.20, f32[8,4,144,24]{3,2,1,0:T(8,128)S(1)} %copy.15), kind=kLoop, calls=%fused_computation | loop fusion | flops 8847360 | bytes 5603328 | tf_op jit(solution)/shard_map/concatenate | solution.py:257
  20.9 0.0 collective-permute-done.below
  20.9 0.0 copy-start.2
  20.9 0.0 collective-permute-done.1.above
  20.9 0.0 copy-start.3
  20.9 0.7 copy-done.2
  21.6 0.1 copy-done.3
  21.7 21.3 %shard_map.100 = (f32[4,144,384]{2,1,0:T(8,128)}, f32[2,144,128]{2,1,0:T(8,128)}, f32[2,144,128]{2,1,0:T(8,128)}) custom-call(f32[2,24,3456]{2,1,0:T(8,128)} %density.1, f32[24,3456]{1,0:T(8,128)} %copy-done.2, f32[24,3456]{1,0:T(8,128)} %copy-done.3, f32[3,2,12,128]{3,2,1,0:T(8,128)} %constant.19.clone.weight, f32[8,4,144,128]{3,2,1,0:T(8,128)} %get-tuple-element.14.gain_a, ...), custom_call_target="tpu_custom_call" | custom-call | tf_op jit(solution)/shard_map/pallas_call | solution.py:243
  43.0 1.1 %collective-permute-start.2 = (f32[2,144,128]{2,1,0:T(8,128)}, f32[2,144,128]{2,1,0:T(8,128)S(1)}, u32[]{:S(2)}, u32[]{:S(2)}) collective-permute-start(f32[2,144,128]{2,1,0:T(8,128)} %get-tuple-element.9), channel_id=1, source_target_pairs={{0,1},{1,2},{2,3},{3,4},{4,5},{5,6},{6,7},{7,0},{8,9},{9,10},{10,1... | collective-permute-start | bytes 442376 | tf_op jit(solution)/shard_map/ppermute | solution.py:263
  44.1 0.9 %collective-permute-start.3 = (f32[2,144,128]{2,1,0:T(8,128)}, f32[2,144,128]{2,1,0:T(8,128)S(1)}, u32[]{:S(2)}, u32[]{:S(2)}) collective-permute-start(f32[2,144,128]{2,1,0:T(8,128)} %get-tuple-element.10), channel_id=1, source_target_pairs={{0,7},{1,0},{2,1},{3,2},{4,3},{5,4},{6,5},{7,6},{8,15},{9,8},{10,9... | collective-permute-start | bytes 442376 | tf_op jit(solution)/shard_map/ppermute | solution.py:263
  45.0 3.3 %collective-permute-done.2.below = f32[2,144,128]{2,1,0:T(8,128)S(1)} collective-permute-done((f32[2,144,128]{2,1,0:T(8,128)}, f32[2,144,128]{2,1,0:T(8,128)S(1)}, u32[]{:S(2)}, u32[]{:S(2)}) %collective-permute-start.2) | collective-permute-done | bytes 147488 | tf_op jit(solution)/shard_map/ppermute | solution.py:263
  48.4 0.0 copy-start.5
  48.4 3.2 %collective-permute-done.3.above = f32[2,144,128]{2,1,0:T(8,128)S(1)} collective-permute-done((f32[2,144,128]{2,1,0:T(8,128)}, f32[2,144,128]{2,1,0:T(8,128)S(1)}, u32[]{:S(2)}, u32[]{:S(2)}) %collective-permute-start.3) | collective-permute-done | bytes 147488 | tf_op jit(solution)/shard_map/ppermute | solution.py:263
  51.6 0.0 copy-start.6
  51.6 0.0 copy-done.5
  51.6 0.6 copy-done.6
  52.2 21.4 %shard_map.101 = f32[2,24,3456]{2,1,0:T(8,128)} custom-call(f32[4,144,384]{2,1,0:T(8,128)} %get-tuple-element.8.before, f32[2,144,128]{2,1,0:T(8,128)} %copy-done.5, f32[2,144,128]{2,1,0:T(8,128)} %copy-done.6, f32[3,2,144,128]{3,2,1,0:T(8,128)} %constant.20.clone.weight, f32[8,4,144,128]{3,2,1,0:T(8,128)} %get-tuple-element.14.gain_a, ...), custom_call_target="tpu_custom_call" | custom-call | tf_op jit(solution)/shard_map/pallas_call | solution.py:243
  (2 shorter events, 0.1 us)
Async XLA Ops:
  0.0 9.1 %copy-start = (f32[8,24,24,24]{3,2,1,0:T(8,128)S(1)}, f32[8,24,24,24]{3,2,1,0:T(8,128)}, u32[]{:S(2)}) copy-start(f32[8,24,24,24]{3,2,1,0:T(8,128)} %param.11) | copy-start | bytes 1327108
  2.1 18.7 %collective-permute-start = (f32[24,3456]{1,0:T(8,128)}, f32[24,3456]{1,0:T(8,128)S(1)}, u32[]{:S(2)}, u32[]{:S(2)}) collective-permute-start(f32[24,3456]{1,0:T(8,128)} %reshape.21), channel_id=1, source_target_pairs={{0,8},{8,16},{16,24},{24,32},{32,40},{40,48},{48,56},{56,64},{64,7... | collective-permute-start | bytes 995336 | tf_op jit(solution)/shard_map/ppermute | solution.py:263
  2.2 18.7 %collective-permute-start.1 = (f32[24,3456]{1,0:T(8,128)S(1)}, f32[24,3456]{1,0:T(8,128)S(1)}, u32[]{:S(2)}, u32[]{:S(2)}) collective-permute-start(f32[24,3456]{1,0:T(8,128)S(1)} %reshape.22), channel_id=1, source_target_pairs={{0,248},{8,0},{16,8},{24,16},{32,24},{40,32},{48,40},{56,48},{64,5... | collective-permute-start | bytes 995336 | tf_op jit(solution)/shard_map/ppermute | solution.py:263
  10.5 1.7 %copy-start.1 = (f32[8,24,24,24]{3,2,1,0:T(8,128)S(1)}, f32[8,24,24,24]{3,2,1,0:T(8,128)}, u32[]{:S(2)}) copy-start(f32[8,24,24,24]{3,2,1,0:T(8,128)} %param.12) | copy-start | bytes 1327108
  13.5 1.0 %copy-start.4 = (f32[24,24,24]{2,1,0:T(8,128)S(1)}, f32[24,24,24]{2,1,0:T(8,128)}, u32[]{:S(2)}) copy-start(f32[24,24,24]{2,1,0:T(8,128)} %param.13) | copy-start | bytes 165892
  20.9 0.7 copy-start.2
  20.9 0.8 %copy-start.3 = (f32[24,3456]{1,0:T(8,128)}, f32[24,3456]{1,0:T(8,128)S(1)}, u32[]{:S(2)}) copy-start(f32[24,3456]{1,0:T(8,128)S(1)} %collective-permute-done.1.above) | copy-start | bytes 995332
  43.0 5.4 %collective-permute-start.2 = (f32[2,144,128]{2,1,0:T(8,128)}, f32[2,144,128]{2,1,0:T(8,128)S(1)}, u32[]{:S(2)}, u32[]{:S(2)}) collective-permute-start(f32[2,144,128]{2,1,0:T(8,128)} %get-tuple-element.9), channel_id=1, source_target_pairs={{0,1},{1,2},{2,3},{3,4},{4,5},{5,6},{6,7},{7,0},{8,9},{9,10},{10,1... | collective-permute-start | bytes 442376 | tf_op jit(solution)/shard_map/ppermute | solution.py:263
  44.1 7.5 %collective-permute-start.3 = (f32[2,144,128]{2,1,0:T(8,128)}, f32[2,144,128]{2,1,0:T(8,128)S(1)}, u32[]{:S(2)}, u32[]{:S(2)}) collective-permute-start(f32[2,144,128]{2,1,0:T(8,128)} %get-tuple-element.10), channel_id=1, source_target_pairs={{0,7},{1,0},{2,1},{3,2},{4,3},{5,4},{6,5},{7,6},{8,15},{9,8},{10,9... | collective-permute-start | bytes 442376 | tf_op jit(solution)/shard_map/ppermute | solution.py:263
  48.4 3.2 %copy-start.5 = (f32[2,144,128]{2,1,0:T(8,128)}, f32[2,144,128]{2,1,0:T(8,128)S(1)}, u32[]{:S(2)}) copy-start(f32[2,144,128]{2,1,0:T(8,128)S(1)} %collective-permute-done.2.below) | copy-start | bytes 442372
  51.6 0.6 copy-start.6
where the time goes:
time: 74 us; the launch traced here: 73.6 us
  Pallas kernels  42.7 us (58%)
  local copies, waits for them, and re-layouts  9.08 us (12%)
  starting transfers between devices  8.96 us (12%)
  waiting for transfers between devices  6.53 us (9%)
  other arithmetic  6.24 us (8%)
    pallas_call x2, Pallas kernels, call(): pl.pallas_call(functools.partial(kernel, groups), grid=(terms,), out_shap...  42.7 us
    ppermute x4, starting transfers between devices, passed_along(): return lax.ppermute(value, axis, pairs)  8.96 us
    ppermute x4, waiting for transfers between devices, passed_along(): return lax.ppermute(value, axis, pairs)  6.53 us
    concatenate x1, other arithmetic, by_parity(): jnp.concatenate([factor] * CELLS, -1)  5.21 us
    reshape x5, local copies, waits for them, and re-layouts, by_parity(): factor.reshape(terms, HALF, 2, HALF, 2, COUNT).transpose(0, 2, 4, 1, 3, 5)  3.67 us
    unnamed x14, local copies, waits for them, and re-layouts  3.15 us
  transfers between devices with their start and end apart: 4, of which 2 were waited for; matrix products, arithmetic and copies ran while one was open for 14% of the time, Pallas kernels for 0%

commit v1 on v0

--- a/solution.py
+++ b/solution.py
@@ -102,10 +102,15 @@
 
 
 def backward(groups, factors, modes, mixed, plane, line):
+    parts = []
     for q in range(4):
         scaled = [modes[q, :, block(g)] * factor(q) for factor in factors for g in range(groups)]
-        moved = line_transform(jnp.concatenate(scaled, 0), line[...])
-        mixed[q, :, : len(scaled) * LANES] = plane_transform(side_by_side(moved, len(scaled)), plane[q])
+        moved = plane_transform(jnp.concatenate(scaled, 1), plane[q])
+        parts += [moved[:, block(i)] for i in range(len(scaled))]
+    moved = line_transform(jnp.concatenate(parts, 0), line[...])
+    count = len(factors) * groups
+    for q in range(4):
+        mixed[q, :, : count * LANES] = side_by_side(moved[q * count * PLACES : (q + 1) * count * PLACES], count)
 
 
 def forward(groups, field, modes, mixed, plane, line):
@@ -251,25 +256,135 @@
     )(*field_args, *gains, *tables)
 
 
-def by_parity(factor):
-    terms = factor.shape[0]
-    factor = factor.reshape(terms, HALF, 2, HALF, 2, COUNT).transpose(0, 2, 4, 1, 3, 5).reshape(terms, 4, PLACES, COUNT)
-    return jnp.pad(jnp.concatenate([factor] * CELLS, -1), ((0, 0),) * 3 + ((0, LANES - CELLS * COUNT),))
-
-
-def passed_along(value, axis, steps):
+def meet(axis):
     count = lax.axis_size(axis)
-    pairs = [(source, (source + steps) % count) for source in range(count)]
-    return lax.ppermute(value, axis, pairs)
+    me = lax.axis_index(axis)
+    after, before = {axis: lax.rem(me + 1, count)}, {axis: lax.rem(me + count - 1, count)}
+    barrier = pltpu.get_barrier_semaphore()
+    for neighbour in (after, before):
+        pl.semaphore_signal(barrier, inc=1, device_id=neighbour, device_id_type=pl.DeviceIdType.MESH)
+    return barrier, after, before
+
+
+def passed(source, target, device, sends, receives, index):
+    return pltpu.make_async_remote_copy(
+        src_ref=source,
+        dst_ref=target,
+        send_sem=sends.at[index],
+        recv_sem=receives.at[index],
+        device_id=device,
+        device_id_type=pl.DeviceIdType.MESH,
+    )
+
+
+def spread(raw, wide, out):
+    used = lax.broadcasted_iota(jnp.int32, (COUNT, LANES), 1) < COUNT
+    for mode in range(COUNT):
+        value = jnp.concatenate([raw[mode], jnp.zeros((COUNT, LANES - COUNT), f32)], 1)
+        value = jnp.where(used, value, 0.0)
+        value = value + pltpu.roll(value, COUNT, 1)
+        wide[mode] = value + pltpu.roll(value, 2 * COUNT, 1)
+    for parity_x in range(2):
+        for parity_y in range(2):
+            rows = [wide[2 * place + parity_x, pl.ds(parity_y, HALF, stride=2), :] for place in range(HALF)]
+            for place in range(0, HALF, 2):
+                out[2 * parity_x + parity_y, place * HALF : (place + 2) * HALF, :] = jnp.concatenate(rows[place : place + 2], 0)
+
+
+def start_kernel(density, gain_a, gain_b, loss, below, above, out_a, out_b, out_loss, *refs):
+    up, down, raw_a, raw_b, raw_loss, wide, made_a, made_b, made_loss, sends, receives, loads, saves, load_loss, save_loss = refs
+    terms = raw_a.shape[0]
+    sides = ((0, gain_a, raw_a, made_a, out_a), (1, gain_b, raw_b, made_b, out_b))
+
+    def load(p, side):
+        i, source, raw, _, _ = sides[side]
+        return pltpu.make_async_copy(source.at[p], raw.at[p], loads.at[i, p])
+
+    def save(p, side):
+        i, _, _, made, out = sides[side]
+        return pltpu.make_async_copy(made.at[p], out.at[p], saves.at[i, p])
+
+    pltpu.make_async_copy(loss, raw_loss, load_loss).start()
+    for side in range(2):
+        lax.fori_loop(0, terms, lambda p, c: (load(p, side).start(), c)[1], 0)
+    barrier, after, before = meet("gx")
+    for c in range(2):
+        up[c * HALF : (c + 1) * HALF, :] = density[c, HALF:, :]
+        down[c * HALF : (c + 1) * HALF, :] = density[c, :HALF, :]
+    pl.semaphore_wait(barrier, 2)
+    forth = passed(up, below, after, sends, receives, 0)
+    back = passed(down, above, before, sends, receives, 1)
+    forth.start()
+    back.start()
+    pltpu.make_async_copy(loss, raw_loss, load_loss).wait()
+    spread(raw_loss, wide, made_loss)
+    pltpu.make_async_copy(made_loss, out_loss, save_loss).start()
+    for side in range(2):
+
+        def one(p, carry):
+            load(p, side).wait()
+            spread(sides[side][2].at[p], wide, sides[side][3].at[p])
+            save(p, side).start()
+            return carry
+
+        lax.fori_loop(0, terms, one, 0)
+    for side in range(2):
+        lax.fori_loop(0, terms, lambda p, c: (save(p, side).wait(), c)[1], 0)
+    pltpu.make_async_copy(made_loss, out_loss, save_loss).wait()
+    forth.wait()
+    back.wait()
+
+
+def start(density, gains_a, gains_b, loss_rates):
+    terms = gains_a.shape[0]
+    rim = jax.ShapeDtypeStruct((COUNT, density.shape[2]), f32)
+    gain = jax.ShapeDtypeStruct((terms, 4, PLACES, LANES), f32)
+    loss = jax.ShapeDtypeStruct((4, PLACES, LANES), f32)
+    anywhere = pl.BlockSpec(memory_space=pl.ANY)
+    dma = pltpu.SemaphoreType.DMA
+    return pl.pallas_call(
+        start_kernel,
+        out_shape=(rim, rim, gain, gain, loss),
+        in_specs=[pl.BlockSpec(memory_space=pltpu.VMEM)] + [anywhere] * 3,
+        out_specs=(anywhere,) * 5,
+        scratch_shapes=[pltpu.VMEM(rim.shape, f32)] * 2
+        + [pltpu.VMEM(a.shape, f32) for a in (gains_a, gains_b, loss_rates)]
+        + [pltpu.VMEM((COUNT, COUNT, LANES), f32)]
+        + [pltpu.VMEM(a.shape, f32) for a in (gain, gain, loss)]
+        + [dma((2,)), dma((2,)), dma((2, terms)), dma((2, terms)), dma, dma],
+        compiler_params=pltpu.CompilerParams(collective_id=0, has_side_effects=True),
+    )(density, gains_a, gains_b, loss_rates)
+
+
+def rim_kernel(lower, upper, below, above, sends, receives):
+    barrier, after, before = meet("gy")
+    pl.semaphore_wait(barrier, 2)
+    forth = passed(upper, below, after, sends, receives, 0)
+    back = passed(lower, above, before, sends, receives, 1)
+    forth.start()
+    back.start()
+    forth.wait()
+    back.wait()
+
+
+def rims(lower, upper):
+    anywhere = pl.BlockSpec(memory_space=pl.ANY)
+    rim = jax.ShapeDtypeStruct(lower.shape, f32)
+    return pl.pallas_call(
+        rim_kernel,
+        out_shape=(rim, rim),
+        in_specs=[anywhere] * 2,
+        out_specs=(anywhere,) * 2,
+        scratch_shapes=[pltpu.SemaphoreType.DMA((2,))] * 2,
+        compiler_params=pltpu.CompilerParams(collective_id=1, has_side_effects=True),
+    )(lower, upper)
 
 
 def body(density, gains_a, gains_b, loss_rates):
     cells_x, count, merged = density.shape
     terms = gains_a.shape[0]
     groups = merged // (2 * count * count)
-    below = passed_along(density[:, HALF:].reshape(count, merged), "gx", 1)
-    above = passed_along(density[:, :HALF].reshape(count, merged), "gx", -1)
-    gains = (by_parity(gains_a), by_parity(gains_b), by_parity(loss_rates[None])[0])
+    below, above, *gains = start(density, gains_a, gains_b, loss_rates)
     tables = tuple(jnp.asarray(t) for t in transform_tables())
     inner = jax.ShapeDtypeStruct((4, PLACES, groups * LANES), f32)
     rim = jax.ShapeDtypeStruct((2, PLACES, LANES), f32)
@@ -277,8 +392,7 @@
     field, lower, upper = call(
         x_kernel, groups, terms, (density, below, above, jnp.asarray(x_weights())), gains, tables, (inner, rim, rim), [swept]
     )
-    below = passed_along(upper, "gy", 1)
-    above = passed_along(lower, "gy", -1)
+    below, above = rims(lower, upper)
     out = jax.ShapeDtypeStruct(density.shape, f32)
     return call(y_kernel, groups, terms, (field, below, above, jnp.asarray(y_weights())), gains, tables, out, [swept])
 

time: 74 us -> 59.4 us (0.80)
  Pallas kernels: 42.7 us -> 59.2 us
  local copies, waits for them, and re-layouts: 9.08 us -> 0 us
  starting transfers between devices: 8.96 us -> 0 us
  waiting for transfers between devices: 6.53 us -> 0 us
  other arithmetic: 6.24 us -> 0 us
    pallas_call x0 -> x2, Pallas kernels: none -> 23.8 us  [the longest x1 14.6 us: start(): pl.pallas_call(start_kernel, out_shape=(rim, rim, gain, gain, loss), in_s...]
    ppermute x4 -> x0, starting transfers between devices: 8.96 us -> none  [passed_along(): return lax.ppermute(value, axis, pairs)]
    pallas_call x2, Pallas kernels: 42.7 us -> 35.4 us  [call(): pl.pallas_call(functools.partial(kernel, groups), grid=(terms,), out_shap...]
    ppermute x4 -> x0, waiting for transfers between devices: 6.53 us -> none  [passed_along(): return lax.ppermute(value, axis, pairs)]
    concatenate x1 -> x0, other arithmetic: 5.21 us -> none  [by_parity(): jnp.concatenate([factor] * CELLS, -1)]
    reshape x7 -> x0, local copies, waits for them, and re-layouts: 4.48 us -> none  [the longest x5 3.67 us: by_parity(): factor.reshape(terms, HALF, 2, HALF, 2, COUNT).transpose(0, 2, 4, 1, 3, 5)]
    unnamed x14 -> x0, local copies, waits for them, and re-layouts: 3.15 us -> none
    slice x1 -> x0, local copies, waits for them, and re-layouts: 1.36 us -> none  [body(): above = passed_along(density[:, :HALF].reshape(count, merged), 'gx', -1)]
  transfers between devices with their start and end apart: 4 -> 0, of which waited for: 2 -> 0; matrix products, arithmetic and copies ran while one was open for 14% -> 0% of each run, Pallas kernels for 0% -> 0%
where the time goes in v1:
time: 59.4 us; the launch traced here: 59.2 us
  Pallas kernels  59.2 us (100%)
    pallas_call x2, Pallas kernels, call(): pl.pallas_call(functools.partial(kernel, groups), grid=(terms,), out_shap...  35.4 us
    pallas_call x1, Pallas kernels, start(): pl.pallas_call(start_kernel, out_shape=(rim, rim, gain, gain, loss), in_s...  14.6 us
    pallas_call x1, Pallas kernels, rims(): pl.pallas_call(rim_kernel, out_shape=(rim, rim), in_specs=[anywhere] * 2,...  9.18 us

profile of v1, /device:TPU:26, one launch (start us, length us, event | category | flops | bytes accessed | tf_op | source)
XLA Modules:
  0.0 59.2 jit_solution(6143999994327436560)
XLA Ops:
  0.0 14.6 %shard_map.100 = (f32[24,3456]{1,0:T(8,128)}, f32[24,3456]{1,0:T(8,128)}, f32[8,4,144,128]{3,2,1,0:T(8,128)}, f32[8,4,144,128]{3,2,1,0:T(8,128)}, f32[4,144,128]{2,1,0:T(8,128)}) custom-call(f32[2,24,3456]{2,1,0:T(8,128)} %density.3, f32[8,24,24,24]{3,2,1,0:T(8,128)} %gain_a.1, f32[8,24,24,24]{3,2,1,0:T(8,128)} %gain_b.1, f32[24,24,24]{2,1,0:T(8,128)} %loss.1), custom_call_target="tpu_custom_call" | custom-call | tf_op jit(solution)/shard_map/pallas_call | solution.py:345
  14.6 17.6 %shard_map.101 = (f32[4,144,384]{2,1,0:T(8,128)}, f32[2,144,128]{2,1,0:T(8,128)}, f32[2,144,128]{2,1,0:T(8,128)}) custom-call(f32[2,24,3456]{2,1,0:T(8,128)} %density.3, f32[24,3456]{1,0:T(8,128)} %get-tuple-element.15.below, f32[24,3456]{1,0:T(8,128)} %get-tuple-element.16.above, f32[3,2,12,128]{3,2,1,0:T(8,128)} %constant.16.clone.weight, ...), custom_call_target="tpu_custom_call" | custom-call | tf_op jit(solution)/shard_map/pallas_call | solution.py:248
  32.2 9.2 %shard_map.102 = (f32[2,144,128]{2,1,0:T(8,128)}, f32[2,144,128]{2,1,0:T(8,128)}) custom-call(f32[2,144,128]{2,1,0:T(8,128)} %get-tuple-element.21.lower, f32[2,144,128]{2,1,0:T(8,128)} %get-tuple-element.22.upper), custom_call_target="tpu_custom_call" | custom-call | tf_op jit(solution)/shard_map/pallas_call | solution.py:373
  41.4 17.8 %shard_map.103 = f32[2,24,3456]{2,1,0:T(8,128)} custom-call(f32[4,144,384]{2,1,0:T(8,128)} %get-tuple-element.20.before, f32[2,144,128]{2,1,0:T(8,128)} %get-tuple-element.23.below, f32[2,144,128]{2,1,0:T(8,128)} %get-tuple-element.24.above, f32[3,2,144,128]{3,2,1,0:T(8,128)} %constant.17.clone.weight, f32[8,4,144,128]{3,2,1,0:T(8,128)} %get-tuple-element.17.gain_a, ...), custom_call_target="tpu_custom_call" | custom-call | tf_op jit(solution)/shard_map/pallas_call | solution.py:248

commit v2 on v1

--- a/solution.py
+++ b/solution.py
@@ -14,6 +14,8 @@
 LANES = 128
 CELLS = 4
 CHUNK = 16
+THIRD = PLACES // 4
+SPARE = LANES - CELLS * COUNT
 collide_step = 0.2
 courant_max = 1.6
 f32 = jnp.float32
@@ -126,38 +128,61 @@
         modes[q] = side_by_side(line_transform(stacked, line[...]), groups)
 
 
-def collide_term(groups, field, total, modes, mixed, gain_a, gain_b, loss, tables):
-    plane_fwd, line_fwd, plane_back, line_back = tables
+def collide(groups, field, total, modes, mixed, arrays, copies, loads, prepare):
+    terms = copies[0].shape[0]
     wide = groups * LANES
-
-    @pl.when(pl.program_id(0) == 0)
-    def _():
-        forward(groups, field, modes, mixed, plane_fwd, line_fwd)
-        backward(groups, [lambda q: loss[q]], modes, mixed, plane_back, line_back)
+    gain_a, gain_b, loss, plane_fwd, line_fwd, plane_back, line_back = copies
+
+    def fixed(i):
+        return pltpu.make_async_copy(arrays[i], copies[i], loads.at[2, i])
+
+    def gain(i, p):
+        return pltpu.make_async_copy(arrays[i].at[p], copies[i].at[p], loads.at[i, p])
+
+    def load(p, carry):
+        gain(0, p).start()
+        gain(1, p).start()
+        return carry
+
+    for i in (3, 4, 2, 5, 6):
+        fixed(i).start()
+    lax.fori_loop(0, terms, load, 0)
+    prepare()
+    fixed(3).wait()
+    fixed(4).wait()
+    forward(groups, field, modes, mixed, plane_fwd, line_fwd)
+    for i in (2, 5, 6):
+        fixed(i).wait()
+    backward(groups, [lambda q: loss[q]], modes, mixed, plane_back, line_back)
+    for start in range(0, PLACES, CHUNK):
+        rows = slice(start, start + CHUNK)
+        parts = butterfly([mixed[q, rows, :wide] for q in range(4)])
+        for q in range(4):
+            total[q, rows, :] = -field[q, rows, :] * parts[q]
+
+    def term(p, carry):
+        gain(0, p).wait()
+        gain(1, p).wait()
+        backward(groups, [lambda q: gain_a[p, q], lambda q: gain_b[p, q]], modes, mixed, plane_back, line_back)
         for start in range(0, PLACES, CHUNK):
             rows = slice(start, start + CHUNK)
-            parts = butterfly([mixed[q, rows, :wide] for q in range(4)])
+            first = butterfly([mixed[q, rows, :wide] for q in range(4)])
+            second = butterfly([mixed[q, rows, wide : 2 * wide] for q in range(4)])
             for q in range(4):
-                total[q, rows, :] = -field[q, rows, :] * parts[q]
-
-    backward(groups, [lambda q: gain_a[0, q], lambda q: gain_b[0, q]], modes, mixed, plane_back, line_back)
-    for start in range(0, PLACES, CHUNK):
-        rows = slice(start, start + CHUNK)
-        first = butterfly([mixed[q, rows, :wide] for q in range(4)])
-        second = butterfly([mixed[q, rows, wide : 2 * wide] for q in range(4)])
-        for q in range(4):
-            total[q, rows, :] += first[q] * second[q]
+                total[q, rows, :] += first[q] * second[q]
+        return carry
+
+    lax.fori_loop(0, terms, term, 0)
 
 
 def piece(y, cell_x, cell_y):
     return cell_y * COUNT * COUNT + y * COUNT
 
 
-def x_kernel(groups, density, below, above, weight, gain_a, gain_b, loss, *refs):
-    tables, (out, lower, upper, swept, field, total, modes, mixed) = refs[:4], refs[4:]
-
-    @pl.when(pl.program_id(0) == 0)
-    def _():
+def x_kernel(groups, density, below, above, weight, *refs):
+    arrays, (out, lower, upper, swept, field, total, modes, mixed, *copies, loads) = refs[:7], refs[7:]
+
+    def prepare():
         neg = [density[c, :HALF, :] for c in range(2)] + [above[:HALF, :], above[HALF:, :]]
         nw = [weight[k, 0, :, :1] for k in range(3)]
         for c in range(2):
@@ -180,22 +205,39 @@
                         parts.append(jnp.zeros((HALF, LANES - CELLS * COUNT), f32))
                         field[2 * half_x + half_y, place * HALF : (place + 1) * HALF, block(g)] = jnp.concatenate(parts, 1)
 
-    collide_term(groups, field, total, modes, mixed, gain_a, gain_b, loss, tables)
-
-    @pl.when(pl.program_id(0) == pl.num_programs(0) - 1)
-    def _():
-        for q in range(4):
-            out[q] = field[q] + collide_step * total[q]
-        for half_x in range(2):
-            lower[half_x] = out[2 * half_x, :, block(0)]
-            upper[half_x] = out[2 * half_x + 1, :, block(groups - 1)]
-
-
-def y_kernel(groups, before, below, above, weight, gain_a, gain_b, loss, *refs):
-    tables, (out, swept, field, total, modes, mixed) = refs[:4], refs[4:]
-
-    @pl.when(pl.program_id(0) == 0)
-    def _():
+    collide(groups, field, total, modes, mixed, arrays, copies, loads, prepare)
+
+    for q in range(4):
+        out[q] = field[q] + collide_step * total[q]
+    for half_x in range(2):
+        pack(out, 2 * half_x, block(0), lower, half_x)
+        pack(out, 2 * half_x + 1, block(groups - 1), upper, half_x)
+
+
+def pack(source, q, lanes, target, half_x):
+    free = lax.broadcasted_iota(jnp.int32, (THIRD, LANES), 1) >= CELLS * COUNT
+    rest = source[q, 3 * THIRD :, lanes]
+    for k in range(3):
+        kept = source[q, k * THIRD : (k + 1) * THIRD, lanes]
+        start = (3 * half_x + k) * THIRD
+        target[start : start + THIRD, :] = jnp.where(free, pltpu.roll(rest, CELLS * COUNT - k * SPARE, 1), kept)
+
+
+def unpack(source, half_x, target):
+    lane = lax.broadcasted_iota(jnp.int32, (THIRD, LANES), 1)
+    rest = jnp.zeros((THIRD, LANES), f32)
+    for k in range(3):
+        start = (3 * half_x + k) * THIRD
+        part = source[start : start + THIRD, :]
+        target[k * THIRD : (k + 1) * THIRD, :] = jnp.where(lane < CELLS * COUNT, part, 0.0)
+        rest = jnp.where(lane // SPARE == k, pltpu.roll(part, LANES - CELLS * COUNT + k * SPARE, 1), rest)
+    target[3 * THIRD :, :] = rest
+
+
+def y_kernel(groups, before, below, above, weight, *refs):
+    arrays, (out, swept, rim, field, total, modes, mixed, *copies, loads) = refs[:7], refs[7:]
+
+    def prepare():
         place = lax.broadcasted_iota(jnp.int32, (PLACES, LANES), 1) // COUNT
         odd = place % 2 == 1
         for half_x in range(2):
@@ -203,7 +245,8 @@
                 q = 2 * half_x + half_y
                 w0, w1, w2 = [weight[k, half_y] for k in range(3)]
                 blocks = [before[q, :, block(g)] for g in range(groups)]
-                blocks = [below[half_x]] + blocks if half_y else blocks + [above[half_x]]
+                unpack(below if half_y else above, half_x, rim)
+                blocks = [rim[...]] + blocks if half_y else blocks + [rim[...]]
                 right = [pltpu.roll(b, COUNT, 1) for b in blocks]
                 left = [pltpu.roll(b, LANES - COUNT, 1) for b in blocks]
                 for g in range(groups):
@@ -215,45 +258,41 @@
                         new = w0 * blocks[g] + w1 * near + w2 * blocks[g + 1]
                     field[q, :, block(g)] = new
 
-    collide_term(groups, field, total, modes, mixed, gain_a, gain_b, loss, tables)
-
-    @pl.when(pl.program_id(0) == pl.num_programs(0) - 1)
-    def _():
-        for q in range(4):
-            field[q] = field[q] + collide_step * total[q]
-        for half_x in range(2):
-            for c in range(2):
-                for g in range(groups):
-                    parts = []
-                    for cell_y in range(2):
-                        for y in range(COUNT):
-                            half_y, place = (0, y) if y < HALF else (1, COUNT - 1 - y)
-                            at = g * LANES + (2 * c + cell_y) * COUNT
-                            parts.append(field[2 * half_x + half_y, place * HALF : (place + 1) * HALF, at : at + COUNT])
-                    wide = 2 * COUNT * COUNT
-                    swept[c, half_x, :HALF, g * wide : (g + 1) * wide] = jnp.concatenate(parts, 1)
+    collide(groups, field, total, modes, mixed, arrays, copies, loads, prepare)
+
+    for q in range(4):
+        field[q] = field[q] + collide_step * total[q]
+    for half_x in range(2):
         for c in range(2):
-            out[c, :HALF, :] = swept[c, 0, :HALF, :]
-            for row in range(HALF):
-                out[c, HALF + row : HALF + row + 1, :] = swept[c, 1, HALF - 1 - row : HALF - row, :]
-
-
-def whole(array):
-    return pl.BlockSpec(array.shape, lambda p: (0,) * array.ndim)
-
-
-def call(kernel, groups, terms, field_args, gains, tables, out_shapes, scratch):
-    gain = pl.BlockSpec((1, 4, PLACES, LANES), lambda p: (p, 0, 0, 0))
+            for g in range(groups):
+                parts = []
+                for cell_y in range(2):
+                    for y in range(COUNT):
+                        half_y, place = (0, y) if y < HALF else (1, COUNT - 1 - y)
+                        at = g * LANES + (2 * c + cell_y) * COUNT
+                        parts.append(field[2 * half_x + half_y, place * HALF : (place + 1) * HALF, at : at + COUNT])
+                wide = 2 * COUNT * COUNT
+                swept[c, half_x, :HALF, g * wide : (g + 1) * wide] = jnp.concatenate(parts, 1)
+    for c in range(2):
+        out[c, :HALF, :] = swept[c, 0, :HALF, :]
+        for row in range(HALF):
+            out[c, HALF + row : HALF + row + 1, :] = swept[c, 1, HALF - 1 - row : HALF - row, :]
+
+
+def call(kernel, groups, field_args, arrays, out_shapes, scratch):
     wide = groups * LANES
+    inside = pl.BlockSpec(memory_space=pltpu.VMEM)
+    terms = arrays[0].shape[0]
     return pl.pallas_call(
         functools.partial(kernel, groups),
-        grid=(terms,),
         out_shape=out_shapes,
-        in_specs=[whole(a) for a in field_args] + [gain, gain, whole(gains[2])] + [whole(t) for t in tables],
-        out_specs=jax.tree.map(whole, out_shapes),
+        in_specs=[inside] * len(field_args) + [pl.BlockSpec(memory_space=pl.ANY)] * len(arrays),
+        out_specs=jax.tree.map(lambda _: inside, out_shapes),
         scratch_shapes=scratch
-        + [pltpu.VMEM((4, PLACES, n * wide), f32) for n in (1, 1, 1, 2)],
-    )(*field_args, *gains, *tables)
+        + [pltpu.VMEM((4, PLACES, n * wide), f32) for n in (1, 1, 1, 2)]
+        + [pltpu.VMEM(a.shape, a.dtype) for a in arrays]
+        + [pltpu.SemaphoreType.DMA((3, max(terms, len(arrays))))],
+    )(*field_args, *arrays)
 
 
 def meet(axis):
@@ -381,20 +420,19 @@
 
 
 def body(density, gains_a, gains_b, loss_rates):
-    cells_x, count, merged = density.shape
-    terms = gains_a.shape[0]
+    count, merged = density.shape[1:]
     groups = merged // (2 * count * count)
     below, above, *gains = start(density, gains_a, gains_b, loss_rates)
-    tables = tuple(jnp.asarray(t) for t in transform_tables())
+    arrays = (*gains, *[jnp.asarray(t) for t in transform_tables()])
     inner = jax.ShapeDtypeStruct((4, PLACES, groups * LANES), f32)
-    rim = jax.ShapeDtypeStruct((2, PLACES, LANES), f32)
+    rim = jax.ShapeDtypeStruct((6 * THIRD, LANES), f32)
     swept = pltpu.VMEM((2, 2, 16, merged), f32)
     field, lower, upper = call(
-        x_kernel, groups, terms, (density, below, above, jnp.asarray(x_weights())), gains, tables, (inner, rim, rim), [swept]
+        x_kernel, groups, (density, below, above, jnp.asarray(x_weights())), arrays, (inner, rim, rim), [swept]
     )
     below, above = rims(lower, upper)
     out = jax.ShapeDtypeStruct(density.shape, f32)
-    return call(y_kernel, groups, terms, (field, below, above, jnp.asarray(y_weights())), gains, tables, out, [swept])
+    return call(y_kernel, groups, (field, below, above, jnp.asarray(y_weights())), arrays, out, [swept, pltpu.VMEM((PLACES, LANES), f32)])
 
 
 def solution(mesh):

time: 59.4 us -> 58.4 us (0.983)
  Pallas kernels: 59.2 us -> 58.3 us
    pallas_call x1, Pallas kernels: 9.18 us -> 8.55 us  [rims(): pl.pallas_call(rim_kernel, out_shape=(rim, rim), in_specs=[anywhere] * 2,...]
where the time goes in v2:
time: 58.4 us; the launch traced here: 58.3 us
  Pallas kernels  58.3 us (100%)
    pallas_call x2, Pallas kernels, call(): pl.pallas_call(functools.partial(kernel, groups), out_shape=out_shapes, i...  35.1 us
    pallas_call x1, Pallas kernels, start(): pl.pallas_call(start_kernel, out_shape=(rim, rim, gain, gain, loss), in_s...  14.6 us
    pallas_call x1, Pallas kernels, rims(): pl.pallas_call(rim_kernel, out_shape=(rim, rim), in_specs=[anywhere] * 2,...  8.55 us

profile of v2, /device:TPU:26, one launch (start us, length us, event | category | flops | bytes accessed | tf_op | source)
XLA Modules:
  0.0 58.3 jit_solution(1246668651016627679)
XLA Ops:
  0.0 14.6 %shard_map.100 = (f32[24,3456]{1,0:T(8,128)}, f32[24,3456]{1,0:T(8,128)}, f32[8,4,144,128]{3,2,1,0:T(8,128)}, f32[8,4,144,128]{3,2,1,0:T(8,128)}, f32[4,144,128]{2,1,0:T(8,128)}) custom-call(f32[2,24,3456]{2,1,0:T(8,128)} %density.3, f32[8,24,24,24]{3,2,1,0:T(8,128)} %gain_a.1, f32[8,24,24,24]{3,2,1,0:T(8,128)} %gain_b.1, f32[24,24,24]{2,1,0:T(8,128)} %loss.1), custom_call_target="tpu_custom_call" | custom-call | tf_op jit(solution)/shard_map/pallas_call | solution.py:384
  14.6 17.2 %shard_map.101 = (f32[4,144,384]{2,1,0:T(8,128)}, f32[216,128]{1,0:T(8,128)}, f32[216,128]{1,0:T(8,128)}) custom-call(f32[2,24,3456]{2,1,0:T(8,128)} %density.3, f32[24,3456]{1,0:T(8,128)} %get-tuple-element.15.below, f32[24,3456]{1,0:T(8,128)} %get-tuple-element.16.above, f32[3,2,12,128]{3,2,1,0:T(8,128)} %constant.16.clone.weight, ...), custom_call_target="tpu_custom_call" | custom-call | tf_op jit(solution)/shard_map/pallas_call | solution.py:286
  31.8 8.5 %shard_map.102 = (f32[216,128]{1,0:T(8,128)}, f32[216,128]{1,0:T(8,128)}) custom-call(f32[216,128]{1,0:T(8,128)} %get-tuple-element.21.lower, f32[216,128]{1,0:T(8,128)} %get-tuple-element.22.upper), custom_call_target="tpu_custom_call" | custom-call | tf_op jit(solution)/shard_map/pallas_call | solution.py:412
  40.3 18.0 %shard_map.103 = f32[2,24,3456]{2,1,0:T(8,128)} custom-call(f32[4,144,384]{2,1,0:T(8,128)} %get-tuple-element.20.before, f32[216,128]{1,0:T(8,128)} %get-tuple-element.23.below, f32[216,128]{1,0:T(8,128)} %get-tuple-element.24.above, f32[3,2,144,128]{3,2,1,0:T(8,128)} %constant.17.clone.weight, f32[8,4,144,128]{3,2,1,0:T(8,128)} %get-tuple-element.17.refs_0_, ...), custom_call_target="tpu_custom_call" | custom-call | tf_op jit(solution)/shard_map/pallas_call | solution.py:286

commit v3 on v2

--- a/solution.py
+++ b/solution.py
@@ -179,39 +179,53 @@
     return cell_y * COUNT * COUNT + y * COUNT
 
 
-def x_kernel(groups, density, below, above, weight, *refs):
-    arrays, (out, lower, upper, swept, field, total, modes, mixed, *copies, loads) = refs[:7], refs[7:]
+def x_kernel(groups, density, ghost_below, ghost_above, weight, *refs):
+    arrays, (out, rim_below, rim_above, swept, lower, upper, sends, receives, save), rest = refs[:7], refs[7:16], refs[16:]
+    field, total, modes, mixed, *copies, loads = rest
+    barrier, after, before = meet("gy")
 
     def prepare():
-        neg = [density[c, :HALF, :] for c in range(2)] + [above[:HALF, :], above[HALF:, :]]
+        neg = [density[c, :HALF, :] for c in range(2)] + [ghost_above[:HALF, :], ghost_above[HALF:, :]]
         nw = [weight[k, 0, :, :1] for k in range(3)]
         for c in range(2):
-            swept[c, 0, :HALF, :] = nw[0] * neg[c] + nw[1] * neg[c + 1] + nw[2] * neg[c + 2]
-        pos = [below[:HALF, :], below[HALF:, :]] + [density[c, HALF:, :] for c in range(2)]
+            swept[c, :HALF, :] = nw[0] * neg[c] + nw[1] * neg[c + 1] + nw[2] * neg[c + 2]
+        pos = [ghost_below[:HALF, :], ghost_below[HALF:, :]] + [density[c, HALF:, :] for c in range(2)]
         pw = [weight[k, 1, :, :1] for k in range(3)]
         for c in range(2):
             new = pw[0] * pos[c + 2] + pw[1] * pos[c + 1] + pw[2] * pos[c]
             for row in range(HALF):
-                swept[c, 1, HALF - 1 - row : HALF - row, :] = new[row : row + 1]
+                swept[c, COUNT - 1 - row : COUNT - row, :] = new[row : row + 1]
         for half_y in range(2):
             for place in range(HALF):
                 y = COUNT - 1 - place if half_y else place
-                for half_x in range(2):
-                    for g in range(groups):
-                        parts = []
-                        for s in range(CELLS):
-                            at = piece(y, s // 2, 2 * g + s % 2)
-                            parts.append(swept[s // 2, half_x, :HALF, at : at + COUNT])
-                        parts.append(jnp.zeros((HALF, LANES - CELLS * COUNT), f32))
-                        field[2 * half_x + half_y, place * HALF : (place + 1) * HALF, block(g)] = jnp.concatenate(parts, 1)
+                for g in range(groups):
+                    parts = []
+                    for s in range(CELLS):
+                        at = piece(y, s // 2, 2 * g + s % 2)
+                        parts.append(swept[s // 2, :, at : at + COUNT])
+                    parts.append(jnp.zeros((COUNT, LANES - CELLS * COUNT), f32))
+                    moved = jnp.concatenate(parts, 1)
+                    rows = slice(place * HALF, (place + 1) * HALF)
+                    field[half_y, rows, block(g)] = moved[:HALF]
+                    field[2 + half_y, rows, block(g)] = moved[HALF:]
 
     collide(groups, field, total, modes, mixed, arrays, copies, loads, prepare)
 
     for q in range(4):
-        out[q] = field[q] + collide_step * total[q]
+        field[q] = field[q] + collide_step * total[q]
     for half_x in range(2):
-        pack(out, 2 * half_x, block(0), lower, half_x)
-        pack(out, 2 * half_x + 1, block(groups - 1), upper, half_x)
+        pack(field, 2 * half_x, block(0), lower, half_x)
+        pack(field, 2 * half_x + 1, block(groups - 1), upper, half_x)
+    pl.semaphore_wait(barrier, 2)
+    forth = passed(upper, rim_below, after, sends, receives, 0)
+    back = passed(lower, rim_above, before, sends, receives, 1)
+    forth.start()
+    back.start()
+    whole = pltpu.make_async_copy(field, out, save)
+    whole.start()
+    whole.wait()
+    forth.wait()
+    back.wait()
 
 
 def pack(source, q, lanes, target, half_x):
@@ -262,24 +276,26 @@
 
     for q in range(4):
         field[q] = field[q] + collide_step * total[q]
-    for half_x in range(2):
+    wide = 2 * COUNT * COUNT
+    for g in range(groups):
+        columns = []
+        for y in range(COUNT):
+            half_y, place = (0, y) if y < HALF else (1, COUNT - 1 - y)
+            rows = slice(place * HALF, (place + 1) * HALF)
+            columns.append(jnp.concatenate([field[half_y, rows, block(g)], field[2 + half_y, rows, block(g)]], 0))
         for c in range(2):
-            for g in range(groups):
-                parts = []
-                for cell_y in range(2):
-                    for y in range(COUNT):
-                        half_y, place = (0, y) if y < HALF else (1, COUNT - 1 - y)
-                        at = g * LANES + (2 * c + cell_y) * COUNT
-                        parts.append(field[2 * half_x + half_y, place * HALF : (place + 1) * HALF, at : at + COUNT])
-                wide = 2 * COUNT * COUNT
-                swept[c, half_x, :HALF, g * wide : (g + 1) * wide] = jnp.concatenate(parts, 1)
+            parts = []
+            for cell_y in range(2):
+                at = (2 * c + cell_y) * COUNT
+                parts += [column[:, at : at + COUNT] for column in columns]
+            swept[c, :, g * wide : (g + 1) * wide] = jnp.concatenate(parts, 1)
     for c in range(2):
-        out[c, :HALF, :] = swept[c, 0, :HALF, :]
+        out[c, :HALF, :] = swept[c, :HALF, :]
         for row in range(HALF):
-            out[c, HALF + row : HALF + row + 1, :] = swept[c, 1, HALF - 1 - row : HALF - row, :]
-
-
-def call(kernel, groups, field_args, arrays, out_shapes, scratch):
+            out[c, HALF + row : HALF + row + 1, :] = swept[c, COUNT - 1 - row : COUNT - row, :]
+
+
+def call(kernel, groups, field_args, arrays, out_shapes, out_space, scratch, **settings):
     wide = groups * LANES
     inside = pl.BlockSpec(memory_space=pltpu.VMEM)
     terms = arrays[0].shape[0]
@@ -287,7 +303,8 @@
         functools.partial(kernel, groups),
         out_shape=out_shapes,
         in_specs=[inside] * len(field_args) + [pl.BlockSpec(memory_space=pl.ANY)] * len(arrays),
-        out_specs=jax.tree.map(lambda _: inside, out_shapes),
+        out_specs=jax.tree.map(lambda _: pl.BlockSpec(memory_space=out_space), out_shapes),
+        compiler_params=pltpu.CompilerParams(**settings),
         scratch_shapes=scratch
         + [pltpu.VMEM((4, PLACES, n * wide), f32) for n in (1, 1, 1, 2)]
         + [pltpu.VMEM(a.shape, a.dtype) for a in arrays]
@@ -388,35 +405,11 @@
         out_specs=(anywhere,) * 5,
         scratch_shapes=[pltpu.VMEM(rim.shape, f32)] * 2
         + [pltpu.VMEM(a.shape, f32) for a in (gains_a, gains_b, loss_rates)]
-        + [pltpu.VMEM((COUNT, COUNT, LANES), f32)]
+        + [pltpu.VMEM((COUNT + 1, COUNT, LANES), f32)]
         + [pltpu.VMEM(a.shape, f32) for a in (gain, gain, loss)]
         + [dma((2,)), dma((2,)), dma((2, terms)), dma((2, terms)), dma, dma],
         compiler_params=pltpu.CompilerParams(collective_id=0, has_side_effects=True),
     )(density, gains_a, gains_b, loss_rates)
-
-
-def rim_kernel(lower, upper, below, above, sends, receives):
-    barrier, after, before = meet("gy")
-    pl.semaphore_wait(barrier, 2)
-    forth = passed(upper, below, after, sends, receives, 0)
-    back = passed(lower, above, before, sends, receives, 1)
-    forth.start()
-    back.start()
-    forth.wait()
-    back.wait()
-
-
-def rims(lower, upper):
-    anywhere = pl.BlockSpec(memory_space=pl.ANY)
-    rim = jax.ShapeDtypeStruct(lower.shape, f32)
-    return pl.pallas_call(
-        rim_kernel,
-        out_shape=(rim, rim),
-        in_specs=[anywhere] * 2,
-        out_specs=(anywhere,) * 2,
-        scratch_shapes=[pltpu.SemaphoreType.DMA((2,))] * 2,
-        compiler_params=pltpu.CompilerParams(collective_id=1, has_side_effects=True),
-    )(lower, upper)
 
 
 def body(density, gains_a, gains_b, loss_rates):
@@ -426,13 +419,14 @@
     arrays = (*gains, *[jnp.asarray(t) for t in transform_tables()])
     inner = jax.ShapeDtypeStruct((4, PLACES, groups * LANES), f32)
     rim = jax.ShapeDtypeStruct((6 * THIRD, LANES), f32)
-    swept = pltpu.VMEM((2, 2, 16, merged), f32)
-    field, lower, upper = call(
-        x_kernel, groups, (density, below, above, jnp.asarray(x_weights())), arrays, (inner, rim, rim), [swept]
-    )
-    below, above = rims(lower, upper)
+    swept = pltpu.VMEM((2, count, merged), f32)
+    dma = pltpu.SemaphoreType.DMA
+    rims = [pltpu.VMEM(rim.shape, f32)] * 2 + [dma((2,)), dma((2,)), dma]
+    before = (density, below, above, jnp.asarray(x_weights()))
+    settings = dict(collective_id=1, has_side_effects=True)
+    field, below, above = call(x_kernel, groups, before, arrays, (inner, rim, rim), pl.ANY, [swept] + rims, **settings)
     out = jax.ShapeDtypeStruct(density.shape, f32)
-    return call(y_kernel, groups, (field, below, above, jnp.asarray(y_weights())), arrays, out, [swept, pltpu.VMEM((PLACES, LANES), f32)])
+    return call(y_kernel, groups, (field, below, above, jnp.asarray(y_weights())), arrays, out, pltpu.VMEM, [swept, pltpu.VMEM((PLACES, LANES), f32)])
 
 
 def solution(mesh):

time: 58.4 us -> 54.8 us (0.938)
  the two profiles are of different devices: /device:TPU:26 before, /device:TPU:10 now
where the time goes in v3:
time: 54.8 us; the launch traced here: 54.6 us
  Pallas kernels  54.6 us (100%)
    pallas_call x2, Pallas kernels, call(): pl.pallas_call(functools.partial(kernel, groups), out_shape=out_shapes, i...  40 us
    pallas_call x1, Pallas kernels, start(): pl.pallas_call(start_kernel, out_shape=(rim, rim, gain, gain, loss), in_s...  14.6 us

profile of v3, /device:TPU:10, one launch (start us, length us, event | category | flops | bytes accessed | tf_op | source)
XLA Modules:
  0.0 54.6 jit_solution(17369858869377001085)
XLA Ops:
  0.0 14.6 %shard_map.100 = (f32[24,3456]{1,0:T(8,128)}, f32[24,3456]{1,0:T(8,128)}, f32[8,4,144,128]{3,2,1,0:T(8,128)}, f32[8,4,144,128]{3,2,1,0:T(8,128)}, f32[4,144,128]{2,1,0:T(8,128)}) custom-call(f32[2,24,3456]{2,1,0:T(8,128)} %density.3, f32[8,24,24,24]{3,2,1,0:T(8,128)} %gain_a.1, f32[8,24,24,24]{3,2,1,0:T(8,128)} %gain_b.1, f32[24,24,24]{2,1,0:T(8,128)} %loss.1), custom_call_target="tpu_custom_call" | custom-call | tf_op jit(solution)/shard_map/pallas_call | solution.py:401
  14.6 22.5 %shard_map.101 = (f32[4,144,384]{2,1,0:T(8,128)}, f32[216,128]{1,0:T(8,128)}, f32[216,128]{1,0:T(8,128)}) custom-call(f32[2,24,3456]{2,1,0:T(8,128)} %density.3, f32[24,3456]{1,0:T(8,128)} %get-tuple-element.13.ghost_below, f32[24,3456]{1,0:T(8,128)} %get-tuple-element.14.ghost_above, f32[3,2,12,128]{3,2,1,0:T(8,128)} %constant.16.clone.weight, ...), custom_call_target="tpu_custom_call" | custom-call | tf_op jit(solution)/shard_map/pallas_call | solution.py:302
  37.1 17.5 %shard_map.102 = f32[2,24,3456]{2,1,0:T(8,128)} custom-call(f32[4,144,384]{2,1,0:T(8,128)} %get-tuple-element.18.before, f32[216,128]{1,0:T(8,128)} %get-tuple-element.19.below, f32[216,128]{1,0:T(8,128)} %get-tuple-element.20.above, f32[3,2,144,128]{3,2,1,0:T(8,128)} %constant.17.clone.weight, f32[8,4,144,128]{3,2,1,0:T(8,128)} %get-tuple-element.15.refs_0_, ...), custom_call_target="tpu_custom_call" | custom-call | tf_op jit(solution)/shard_map/pallas_call | solution.py:302

commit v4 on v3

--- a/solution.py
+++ b/solution.py
@@ -347,9 +347,13 @@
                 out[2 * parity_x + parity_y, place * HALF : (place + 2) * HALF, :] = jnp.concatenate(rows[place : place + 2], 0)
 
 
-def start_kernel(density, gain_a, gain_b, loss, below, above, out_a, out_b, out_loss, *refs):
-    up, down, raw_a, raw_b, raw_loss, wide, made_a, made_b, made_loss, sends, receives, loads, saves, load_loss, save_loss = refs
+def start_kernel(source, gain_a, gain_b, loss, below, above, out_a, out_b, out_loss, *refs):
+    density, up, down, raw_a, raw_b, raw_loss, wide, made_a, made_b, made_loss, *sems = refs
+    sends, receives, loads, saves, load_loss, save_loss, load_density = sems
     terms = raw_a.shape[0]
+    barrier, after, before = meet("gx")
+    whole = pltpu.make_async_copy(source, density, load_density)
+    whole.start()
     sides = ((0, gain_a, raw_a, made_a, out_a), (1, gain_b, raw_b, made_b, out_b))
 
     def load(p, side):
@@ -363,7 +367,7 @@
     pltpu.make_async_copy(loss, raw_loss, load_loss).start()
     for side in range(2):
         lax.fori_loop(0, terms, lambda p, c: (load(p, side).start(), c)[1], 0)
-    barrier, after, before = meet("gx")
+    whole.wait()
     for c in range(2):
         up[c * HALF : (c + 1) * HALF, :] = density[c, HALF:, :]
         down[c * HALF : (c + 1) * HALF, :] = density[c, :HALF, :]
@@ -401,13 +405,13 @@
     return pl.pallas_call(
         start_kernel,
         out_shape=(rim, rim, gain, gain, loss),
-        in_specs=[pl.BlockSpec(memory_space=pltpu.VMEM)] + [anywhere] * 3,
+        in_specs=[anywhere] * 4,
         out_specs=(anywhere,) * 5,
-        scratch_shapes=[pltpu.VMEM(rim.shape, f32)] * 2
+        scratch_shapes=[pltpu.VMEM(density.shape, f32)] + [pltpu.VMEM(rim.shape, f32)] * 2
         + [pltpu.VMEM(a.shape, f32) for a in (gains_a, gains_b, loss_rates)]
         + [pltpu.VMEM((COUNT + 1, COUNT, LANES), f32)]
         + [pltpu.VMEM(a.shape, f32) for a in (gain, gain, loss)]
-        + [dma((2,)), dma((2,)), dma((2, terms)), dma((2, terms)), dma, dma],
+        + [dma((2,)), dma((2,)), dma((2, terms)), dma((2, terms)), dma, dma, dma],
         compiler_params=pltpu.CompilerParams(collective_id=0, has_side_effects=True),
     )(density, gains_a, gains_b, loss_rates)
 

time: 54.8 us -> 53.6 us (0.978)
  Pallas kernels: 54.6 us -> 53.5 us
    pallas_call x1, Pallas kernels: 14.6 us -> 13.5 us  [start(): pl.pallas_call(start_kernel, out_shape=(rim, rim, gain, gain, loss), in_s...]
where the time goes in v4:
time: 53.6 us; the launch traced here: 53.5 us
  Pallas kernels  53.5 us (100%)
    pallas_call x2, Pallas kernels, call(): pl.pallas_call(functools.partial(kernel, groups), out_shape=out_shapes, i...  40 us
    pallas_call x1, Pallas kernels, start(): pl.pallas_call(start_kernel, out_shape=(rim, rim, gain, gain, loss), in_s...  13.5 us

profile of v4, /device:TPU:10, one launch (start us, length us, event | category | flops | bytes accessed | tf_op | source)
XLA Modules:
  0.0 53.5 jit_solution(6047445101470615160)
XLA Ops:
  0.0 13.5 %shard_map.100 = (f32[24,3456]{1,0:T(8,128)}, f32[24,3456]{1,0:T(8,128)}, f32[8,4,144,128]{3,2,1,0:T(8,128)}, f32[8,4,144,128]{3,2,1,0:T(8,128)}, f32[4,144,128]{2,1,0:T(8,128)}) custom-call(f32[2,24,3456]{2,1,0:T(8,128)} %density.1, f32[8,24,24,24]{3,2,1,0:T(8,128)} %gain_a.1, f32[8,24,24,24]{3,2,1,0:T(8,128)} %gain_b.1, f32[24,24,24]{2,1,0:T(8,128)} %loss.1), custom_call_target="tpu_custom_call" | custom-call | tf_op jit(solution)/shard_map/pallas_call | solution.py:405
  13.5 22.5 %shard_map.101 = (f32[4,144,384]{2,1,0:T(8,128)}, f32[216,128]{1,0:T(8,128)}, f32[216,128]{1,0:T(8,128)}) custom-call(f32[2,24,3456]{2,1,0:T(8,128)} %density.1, f32[24,3456]{1,0:T(8,128)} %get-tuple-element.13.ghost_below, f32[24,3456]{1,0:T(8,128)} %get-tuple-element.14.ghost_above, f32[3,2,12,128]{3,2,1,0:T(8,128)} %constant.16.clone.weight, ...), custom_call_target="tpu_custom_call" | custom-call | tf_op jit(solution)/shard_map/pallas_call | solution.py:302
  36.0 17.5 %shard_map.102 = f32[2,24,3456]{2,1,0:T(8,128)} custom-call(f32[4,144,384]{2,1,0:T(8,128)} %get-tuple-element.18.before, f32[216,128]{1,0:T(8,128)} %get-tuple-element.19.below, f32[216,128]{1,0:T(8,128)} %get-tuple-element.20.above, f32[3,2,144,128]{3,2,1,0:T(8,128)} %constant.17.clone.weight, f32[8,4,144,128]{3,2,1,0:T(8,128)} %get-tuple-element.15.refs_0_, ...), custom_call_target="tpu_custom_call" | custom-call | tf_op jit(solution)/shard_map/pallas_call | solution.py:302
